TPU v7x, 32 devices: a whole 2x2x4 slice. The times are simulated.
32 devices in a mesh: seq: 8 (over y, x, core), head: 4 (over z).
Axes of the slice: x: 2, y: 2, z: 4, core: 2. Of those that a mesh axis runs over, the one named last changes fastest.
Arguments:
- positions: int32 [4096], P('seq'), may hold values from 65535 to 73725, as said below
- queries: bfloat16 [4096, 32, 128], P('seq', 'head'), may hold values from -16 to 16
- keys: bfloat16 [4096, 16, 128], P('seq', 'head'), may hold values from -16 to 16
- values: bfloat16 [4096, 16, 128], P('seq', 'head'), may hold values from -6 to 6
- out_weight: bfloat16 [4096, 5376], P('head', 'seq'), may hold values from -0.125 to 0.125
- post_gain: float32 [5376], P('head'), may hold values from 0.25 to 1.75
- residual: bfloat16 [4096, 5376], P('seq', 'head'), may hold values from -6 to 6
Outputs:
- layer_out: bfloat16 [4096, 5376], P('seq', 'head')
Inputs may be any that keep to these rules, and one draw needn't show every extreme that they name: `positions`: strictly rising, by 1 or 2 from one token to the next; the last token's position is the most.
All inputs are finite; a program needn't handle non-finite values.
Results may differ from a plain program's by a relative error of at most 0.015.
Values may be sent and summed in bfloat16 or wider, within the bound.
A program may use at most 128 MiB of HBM per device.

v0:
```python
import functools

import jax
import jax.numpy as jnp
from jax import lax
from jax.experimental import pallas as pl
from jax.experimental.pallas import tpu as pltpu
from jax.sharding import PartitionSpec as P

D = 5376
QUERY_HEADS = 32
KEY_VALUE_HEADS = 16
VISIBLE_SPAN = 1024


EPS = 1e-06
SCALE = 168.0 ** (-0.5)
LOG2E = 1.4426950408889634
MASKED = -1e30
TILE = 256
LANES = 128
MESH = pl.DeviceIdType.MESH


def passed_along(value, axis, steps):
    count = lax.axis_size(axis)
    initial, last = (max(0, -steps), min(count, count - steps))
    return lax.ppermute(value, axis, [(source, source + steps) for source in range(initial, last)])


def rotate(x, positions):
    half = x.shape[-1] // 2
    inverse = 10000.0 ** (-2.0 * jnp.arange(half, dtype=jnp.float32) / x.shape[-1])
    angle = positions.astype(jnp.float32)[:, None] * inverse[None, :]
    cosine = jnp.concatenate([jnp.cos(angle), jnp.cos(angle)], -1)[:, None, :]
    sine = jnp.concatenate([jnp.sin(angle), jnp.sin(angle)], -1)[:, None, :]
    source = x.astype(jnp.float32)
    turned = jnp.concatenate([-source[..., half:], source[..., :half]], -1)
    return (source * cosine + turned * sine).astype(jnp.bfloat16)


def layer_kernel(
    n_seq, n_head, kv_heads, groups, reach,
    q_ref, k_ref, v_ref, w_ref, gain_ref, res_ref, out_ref,
    k_ext, v_ext, stage, w_all, ctx, acc, squares,
    halo_send, halo_recv, pass_send, a_send, a_recv, a_local, c_send, c_recv, c_local, b_send, b_recv, relay_send, relay_recv,
    up_send, down_send, ctx_recv, sq_send, sq_recv,
):
    me = lax.axis_index("seq")
    z = lax.axis_index("head")
    rows = k_ref.shape[1]
    size = k_ref.shape[2]
    feats = w_ref.shape[0]
    sub = n_seq // n_head
    span = reach * rows
    sibling = me + 1 - 2 * lax.rem(me, 2)
    pair = groups * size

    def remote(src, dst, send, recv, device):
        return pltpu.make_async_remote_copy(
            src_ref=src, dst_ref=dst, send_sem=send, recv_sem=recv,
            device_id=device, device_id_type=MESH,
        )

    def halo(dist, g, kv, target):
        at = pl.ds(span - dist * rows, rows)
        if kv == 0:
            src, dst = k_ref.at[g], k_ext.at[g, at, :]
        else:
            src, dst = v_ref.at[g], v_ext.at[g, :, at]
        return remote(src, dst, halo_send.at[dist - 1, g, kv], halo_recv.at[dist - 1, g, kv], (target, z))

    def piece(p, source, target):
        return remote(
            w_ref.at[:, pl.ds(pl.multiple_of(p * LANES, LANES), LANES)], stage.at[source],
            a_send.at[p], a_recv.at[source], (target, z),
        )

    def own_piece():
        return pltpu.make_async_copy(
            w_ref.at[:, pl.ds(pl.multiple_of(me * LANES, LANES), LANES)], stage.at[me], a_local
        )

    def climb(h, source, target):
        return remote(
            stage.at[pl.ds(h * sub, sub)], w_all.at[me, source],
            c_send.at[h], c_recv.at[source], (me, target),
        )

    def own_climb():
        return pltpu.make_async_copy(stage.at[pl.ds(z * sub, sub)], w_all.at[me, z], c_local)

    even = lax.rem(me, 2) == 0

    def passed_on(g, kv):
        near, far = pl.ds(span - rows, rows), pl.ds(span - 2 * rows, rows)
        if kv == 0:
            src, dst = k_ext.at[g, near, :], k_ext.at[g, far, :]
        else:
            src, dst = v_ext.at[g, :, near], v_ext.at[g, :, far]
        return remote(src, dst, pass_send.at[g, kv], halo_recv.at[1, g, kv], (me + 1, z))

    def start_halo(g):
        @pl.when(me + 1 < n_seq)
        def _():
            halo(1, g, 0, me + 1).start()
            halo(1, g, 1, me + 1).start()

        @pl.when(jnp.logical_and(even, me + 2 < n_seq))
        def _():
            halo(2, g, 0, me + 2).start()
            halo(2, g, 1, me + 2).start()

    start_halo(0)
    own_piece().start()
    for d in range(1, n_seq):
        other = lax.rem(me + d, n_seq)
        piece(other, me, other).start()

    for g in range(1, kv_heads):
        start_halo(g)

    for dist in range(1, reach + 1):
        @pl.when(me < dist)
        def _():
            at = pl.ds(span - dist * rows, rows)
            k_ext[:, at, :] = jnp.zeros((kv_heads, rows, size), jnp.bfloat16)
            v_ext[:, :, at] = jnp.zeros((kv_heads, size, rows), jnp.bfloat16)
    k_ext[:, pl.ds(span, rows), :] = k_ref[...]
    v_ext[:, :, pl.ds(span, rows)] = v_ref[...]

    def chunk(r, g):
        return ctx.at[r, pl.ds(g * pair, pair), :]

    def ctx_up(r, g):
        return remote(chunk(r, g), chunk(r, g), up_send.at[r, g], ctx_recv.at[r, g], (me, z + 1))

    def ctx_down(r, g):
        return remote(chunk(r, g), chunk(r, g), down_send.at[r, g], ctx_recv.at[r, g], (me, z - 1))

    def arrive(dist, g, then_send):
        @pl.when(z - dist >= 0)
        def _():
            r = z - dist
            ctx_up(r, g).wait_recv()
            if then_send:
                @pl.when(z + 1 < n_head)
                def _():
                    ctx_up(r, g).start()

        @pl.when(z + dist < n_head)
        def _():
            r = z + dist
            ctx_down(r, g).wait_recv()
            if then_send:
                @pl.when(z - 1 >= 0)
                def _():
                    ctx_down(r, g).start()

    offsets = n_seq // 2

    def spread(m, source, target):
        return remote(w_all.at[source], w_all.at[source], b_send.at[m], b_recv.at[m], (target, z))

    def relay(m, source):
        return remote(w_all.at[source], w_all.at[source], relay_send.at[m], relay_recv.at[m], (sibling, z))

    def start_climb():
        own_piece().wait()
        for d in range(1, n_seq):
            source = lax.rem(me - d + n_seq, n_seq)
            piece(source, source, me).wait_recv()
        own_climb().start()
        for d in range(1, n_head):
            h = lax.rem(z + d, n_head)
            climb(h, z, h).start()

    def start_spread():
        own_climb().wait()
        for d in range(1, n_head):
            climb(0, lax.rem(z + d, n_head), z).wait_recv()
        for m in range(1, offsets):
            spread(m, me, lax.rem(me + 2 * m, n_seq)).start()
        relay(0, me).start()

    blocks = span // TILE + 1
    for g in range(kv_heads):
        for dist in range(1, reach + 1):
            @pl.when(me >= dist)
            def _():
                halo(dist, g, 0, me).wait_recv()
                halo(dist, g, 1, me).wait_recv()
                if dist == 1:
                    @pl.when(even)
                    def _():
                        passed_on(g, 0).start()
                        passed_on(g, 1).start()

        @pl.loop(0, rows // TILE)
        def _(t):
            first = pl.multiple_of(t * TILE, TILE)
            q = jnp.concatenate([q_ref[g * groups + i, pl.ds(first, TILE), :] for i in range(groups)], 0)
            row = lax.broadcasted_iota(jnp.int32, (TILE, groups * TILE), 0)
            col = lax.rem(lax.broadcasted_iota(jnp.int32, (TILE, groups * TILE), 1), TILE)
            scores = []
            top = None
            for b in range(blocks):
                s = lax.dot_general(
                    k_ext[g, pl.ds(first + b * TILE, TILE), :], q,
                    (((1,), (1,)), ((), ())), preferred_element_type=jnp.float32,
                )
                valid = me * rows + first + b * TILE - span >= 0
                if b == 0:
                    s = jnp.where(jnp.logical_and(row > col, valid), s, MASKED)
                elif b == blocks - 1:
                    s = jnp.where(row <= col, s, MASKED)
                else:
                    s = jnp.where(valid, s, MASKED)
                scores.append(s)
                high = jnp.max(s, axis=0, keepdims=True)
                top = high if top is None else jnp.maximum(top, high)
            shift = top * (SCALE * LOG2E)
            total = None
            mixed = None
            for b in range(blocks):
                w = jnp.exp2(scores[b] * (SCALE * LOG2E) - shift)
                part_sum = jnp.sum(w, axis=0, keepdims=True)
                total = part_sum if total is None else total + part_sum
                o = jnp.dot(
                    v_ext[g, :, pl.ds(pl.multiple_of(first + b * TILE, TILE), TILE)], w.astype(jnp.bfloat16),
                    preferred_element_type=jnp.float32,
                )
                mixed = o if mixed is None else mixed + o
            result = (mixed / total).astype(jnp.bfloat16)
            for i in range(groups):
                ctx[z, pl.ds((g * groups + i) * size, size), pl.ds(first, TILE)] = result[:, i * TILE : (i + 1) * TILE]

        @pl.when(z + 1 < n_head)
        def _():
            ctx_up(z, g).start()

        @pl.when(z >= 1)
        def _():
            ctx_down(z, g).start()
        if g == 0:
            start_climb()
        if g >= 1:
            arrive(1, g - 1, True)
    start_spread()

    arrive(1, kv_heads - 1, True)
    for dist in range(2, n_head):
        for g in range(kv_heads):
            arrive(dist, g, dist + 1 < n_head)

    tile = next(t for t in range(256, 0, -16) if feats % t == 0)

    def project(p, init):
        block = jnp.concatenate(
            [ctx[r, pl.ds(pl.multiple_of(p * LANES, LANES), LANES), :] for r in range(n_head)], 0
        )
        for j in range(sub):
            @pl.loop(0, feats // tile)
            def _(t):
                at = pl.ds(pl.multiple_of(t * tile, tile), tile)
                w = jnp.concatenate([w_all[p, r, j, at, :] for r in range(n_head)], 1)
                got = jnp.dot(w, block, preferred_element_type=jnp.float32)
                if init:
                    acc[j, at, :] = got
                else:
                    acc[j, at, :] += got

    project(me, True)
    relay(0, sibling).wait_recv()
    project(sibling, False)
    for m in range(1, offsets):
        source = lax.rem(me - 2 * m + n_seq, n_seq)
        spread(m, source, me).wait_recv()
        relay(m, source).start()
        project(source, False)
    for m in range(1, offsets):
        source = lax.rem(sibling - 2 * m + n_seq, n_seq)
        relay(m, source).wait_recv()
        project(source, False)

    mine = jnp.zeros((8, rows), jnp.float32)
    for j in range(sub):
        value = acc[j]
        mine = mine + jnp.sum((value * value).reshape(feats // 8, 8, rows), axis=0)
    squares[0] = mine

    def sq(d, target):
        return remote(squares.at[0], squares.at[d], sq_send.at[d - 1], sq_recv.at[d - 1], (me, target))

    for d in range(1, n_head):
        sq(d, lax.rem(z + d, n_head)).start()
    for d in range(1, n_head):
        sq(d, z).wait_recv()
    whole = jnp.sum(jnp.sum(squares[...], axis=0), axis=0, keepdims=True)
    inverse = lax.rsqrt(whole / (n_head * sub * feats) + EPS)
    for j in range(sub):
        at = pl.ds(j * feats, feats)
        out_ref[at, :] = (
            res_ref[at, :].astype(jnp.float32) + gain_ref[at, :] * (acc[j] * inverse)
        ).astype(jnp.bfloat16)

    for d in range(1, n_head):
        sq(d, z).wait_send()
    for g in range(kv_heads):
        for dist in range(1, reach + 1):
            leaves = me + dist < n_seq
            if dist == 2:
                leaves = jnp.logical_and(even, leaves)

            @pl.when(leaves)
            def _():
                halo(dist, g, 0, me).wait_send()
                halo(dist, g, 1, me).wait_send()

        @pl.when(jnp.logical_and(even, me >= 1))
        def _():
            passed_on(g, 0).wait_send()
            passed_on(g, 1).wait_send()
    for d in range(1, n_seq):
        piece(lax.rem(me + d, n_seq), me, me).wait_send()
    for d in range(1, n_head):
        climb(lax.rem(z + d, n_head), z, z).wait_send()
    for m in range(1, offsets):
        spread(m, me, me).wait_send()
        relay(m, lax.rem(me - 2 * m + n_seq, n_seq)).wait_send()
    relay(0, me).wait_send()
    for g in range(kv_heads):
        for dist in range(n_head - 1):
            @pl.when(jnp.logical_and(z - dist >= 0, z + 1 < n_head))
            def _():
                ctx_up(z - dist, g).wait_send()

            @pl.when(jnp.logical_and(z + dist < n_head, z >= 1))
            def _():
                ctx_down(z + dist, g).wait_send()


def fits(rows, heads_rows, kv_heads, feats, n_seq, n_head):
    return (
        n_seq % 2 == 0
        and n_seq % n_head == 0
        and heads_rows == n_seq * LANES
        and rows % TILE == 0
        and VISIBLE_SPAN == 2 * rows
        and kv_heads >= 2
        and feats % 16 == 0
    )


def fused(positions, queries, keys, values, out_weight, post_gain, residual):
    n_seq, n_head = lax.axis_size("seq"), lax.axis_size("head")
    rows, kv_heads, size = keys.shape
    groups = queries.shape[1] // kv_heads
    feats = out_weight.shape[1]
    width = residual.shape[1]
    sub = n_seq // n_head
    reach = VISIBLE_SPAN // rows
    q = rotate(queries, positions).transpose(1, 0, 2)
    k = rotate(keys, positions).transpose(1, 0, 2)
    v = values.transpose(1, 2, 0)
    bf16, f32 = jnp.bfloat16, jnp.float32
    dma = pltpu.SemaphoreType.DMA
    spec = pl.BlockSpec(memory_space=pltpu.VMEM)
    out = pl.pallas_call(
        functools.partial(layer_kernel, n_seq, n_head, kv_heads, groups, reach),
        out_shape=jax.ShapeDtypeStruct((width, rows), bf16),
        in_specs=[spec] * 6,
        out_specs=spec,
        scratch_shapes=[
            pltpu.VMEM((kv_heads, (reach + 1) * rows, size), bf16),
            pltpu.VMEM((kv_heads, size, (reach + 1) * rows), bf16),
            pltpu.VMEM((n_seq, feats, LANES), bf16),
            pltpu.VMEM((n_seq, n_head, sub, feats, LANES), bf16),
            pltpu.VMEM((n_head, kv_heads * groups * size, rows), bf16),
            pltpu.VMEM((sub, feats, rows), f32),
            pltpu.VMEM((n_head, 8, rows), f32),
            dma((reach, kv_heads, 2)), dma((reach, kv_heads, 2)), dma((kv_heads, 2)),
            dma((n_seq,)), dma((n_seq,)), dma, dma((n_head,)), dma((n_head,)), dma,
            dma((n_seq // 2,)), dma((n_seq // 2,)), dma((n_seq // 2,)), dma((n_seq // 2,)),
            dma((n_head, kv_heads)), dma((n_head, kv_heads)), dma((n_head, kv_heads)),
            dma((n_head,)), dma((n_head,)),
        ],
        compiler_params=pltpu.CompilerParams(has_side_effects=True, vmem_limit_bytes=60 * 1024 * 1024),
    )(q, k, v, out_weight.T, post_gain[:, None], residual.T)
    return out.T


def general(positions, queries, keys, values, out_weight, post_gain, residual):
    rows = queries.shape[0]
    kv_heads = keys.shape[1]
    query_groups = QUERY_HEADS // KEY_VALUE_HEADS
    q_rot = rotate(queries, positions)
    stacked = jnp.stack([rotate(keys, positions), values], 0)
    reach = (VISIBLE_SPAN + rows - 2) // rows
    pieces = []
    carried = stacked
    for hop in range(reach):
        carried = passed_along(carried, "seq", 1)
        pieces.insert(0, carried)
    extended = jnp.concatenate(pieces + [stacked], axis=1)
    extra = extended.shape[1] - rows
    anchor = lax.axis_index("seq") * rows
    tile_rows = q_rot.reshape(rows, kv_heads, query_groups, -1)
    scores = jnp.einsum("qhgd,khd->hgqk", tile_rows, extended[0], preferred_element_type=jnp.float32) * SCALE
    query_index = anchor + jnp.arange(rows, dtype=jnp.int32)
    key_index = anchor - extra + jnp.arange(extra + rows, dtype=jnp.int32)
    gap = query_index[:, None] - key_index[None, :]
    allowed = (gap >= 0) & (gap < VISIBLE_SPAN) & (key_index[None, :] >= 0)
    scores = jnp.where(allowed, scores, MASKED)
    top = jnp.max(scores, axis=-1, keepdims=True)
    weights = jnp.exp(scores - top)
    probs = (weights / jnp.sum(weights, axis=-1, keepdims=True)).astype(jnp.bfloat16)
    context = jnp.einsum("hgqk,khd->qhgd", probs, extended[1], preferred_element_type=jnp.float32)
    context = context.astype(jnp.bfloat16).reshape(rows, -1)
    partial_value = jnp.dot(
        context,
        lax.all_gather(out_weight, "seq", axis=1, tiled=True),
        preferred_element_type=jnp.float32,
    )
    attended = lax.psum_scatter(
        partial_value.astype(jnp.bfloat16), "head", scatter_dimension=1, tiled=True
    ).astype(jnp.float32)
    squares = lax.psum(jnp.sum(attended * attended, axis=1), "head")
    scaled = attended * lax.rsqrt(squares / D + EPS)[:, None]
    result = residual.astype(jnp.float32) + post_gain[None, :] * scaled
    return result.astype(jnp.bfloat16)


def on_device(positions, queries, keys, values, out_weight, post_gain, residual):
    n_seq, n_head = lax.axis_size("seq"), lax.axis_size("head")
    rows, kv_heads, _ = keys.shape
    body = fused if fits(rows, out_weight.shape[0], kv_heads, out_weight.shape[1], n_seq, n_head) else general
    return body(positions, queries, keys, values, out_weight, post_gain, residual)


def solution(mesh):
    return jax.shard_map(
        on_device,
        mesh=mesh,
        in_specs=(
            P("seq"),
            P("seq", "head", None),
            P("seq", "head", None),
            P("seq", "head", None),
            P("head", "seq"),
            P("head"),
            P("seq", "head"),
        ),
        out_specs=P("seq", "head"),
        check_vma=False,
    )
```

profile of v0, /device:TPU:0, one launch (start us, length us, event | category | flops | bytes accessed | tf_op | source)
XLA Modules:
  0.0 165.1 jit_solution(3722242482954290089)
XLA Ops:
  0.0 1.4 copy_convert_fusion
  1.4 0.0 copy-start.4
  1.4 0.7 slice_negate_fusion
  2.1 0.0 copy-start
  2.1 0.0 copy-done.4
  2.1 1.0 multiply_cosine_fusion
  3.1 0.2 pad_maximum_fusion
  3.3 0.0 copy-done
  3.3 0.0 copy-start.1
  3.4 1.7 %fusion.2.q_ref = bf16[8,512,128]{2,1,0:T(8,128)(2,1)} fusion(f32[512,8,64]{2,0,1:T(8,128)S(1)} %get-tuple-element.6, f32[512,8,64]{2,0,1:T(8,128)S(1)} %get-tuple-element.5, f32[512,128]{1,0:T(8,128)S(1)} %get-tuple-element.12, f32[512,128]{1,0:T(8,128)S(1)} %get-tuple-element.11, bf16[512,8,128]{2,1,0:T(8,128)(2,1)S(1)} %copy-done), kind=kLoop, calls=%fused_computation.4 | loop fusion | flops 3145728 | bytes 4718592 | tf_op jit(solution)/shard_map/transpose | solution.py:363
  5.1 0.0 copy-done.1
  5.1 0.1 copy_convert_fusion.1
  5.1 0.3 slice_negate_fusion.1
  5.5 0.0 copy-start.2
  5.5 0.0 copy-start.3
  5.5 1.2 fusion.5.k_ref
  6.7 0.0 copy-done.2
  6.7 1.1 copy.13
  7.9 0.0 copy-done.3
  7.9 1.1 broadcast_in_dim.3.gain_ref
  9.0 153.6 %shard_map.73 = bf16[1344,512]{1,0:T(8,128)(2,1)} custom-call(bf16[8,512,128]{2,1,0:T(8,128)(2,1)} %fusion.2.q_ref, bf16[4,512,128]{2,1,0:T(8,128)(2,1)} %fusion.5.k_ref, bf16[4,128,512]{2,1,0:T(8,128)(2,1)} %bitcast.9, bf16[672,1024]{1,0:T(8,128)(2,1)} %bitcast.10, f32[1344,1]{1,0:T(8,128)} %broadcast_in_dim.3.gain_ref, bf16[1344,512]{1,0:T(8,128)(2,1)} %bitcast.11), custom_call_target="tpu_custom_call" | custom-call | tf_op jit(solution)/shard_map/pallas_call | solution.py:369
  162.6 2.5 %copy.22 = bf16[512,1344]{0,1:T(8,128)(2,1)} copy(bf16[512,1344]{0,1:T(8,128)(2,1)} %bitcast.8) | data formatting | bytes 2752512
  (2 shorter events, 0.0 us)
Async XLA Ops:
  1.4 0.8 copy-start.4
  2.1 1.2 copy-start
  3.3 1.7 %copy-start.1 = (bf16[512,4,128]{2,1,0:T(4,128)(2,1)S(1)}, bf16[512,4,128]{2,1,0:T(4,128)(2,1)}, u32[]{:S(2)}) copy-start(bf16[512,4,128]{2,1,0:T(4,128)(2,1)} %param.9) | copy-start | bytes 1572868
  5.5 1.2 copy-start.2
  5.5 2.4 %copy-start.3 = (f32[1344]{0:T(1024)S(1)}, f32[1344]{0:T(1024)}, u32[]{:S(2)}) copy-start(f32[1344]{0:T(1024)} %param.12) | copy-start | bytes 16132
where the time goes:
time: 165 us
  Pallas kernels  154 us (93%)
  other arithmetic  6.6 us (4%)
  local copies, waits for them, and re-layouts  4.78 us (3%)
    pallas_call x1, Pallas kernels, fused(): pl.pallas_call(functools.partial(layer_kernel, n_seq, n_head, kv_heads, g...  154 us
    unnamed x12, local copies, waits for them, and re-layouts  3.67 us

commit v1 on v0

--- a/solution.py
+++ b/solution.py
@@ -20,6 +20,17 @@
 TILE = 256
 LANES = 128
 MESH = pl.DeviceIdType.MESH
+LAUNCH = (
+    "Z0", "Z1", "Z2", "Z3", "Z4", "Z5", "Z6", "H0", "H1", "H2", "H3",
+)
+PLAN = (
+    "T6", "T0", "T1", "T2", "T3", "T4", "T5", "C0", "A0", "A1", "C1", "A2",
+    "A3", "C2", "C3", "R10", "R11", "R12", "R13", "X0", "Y0", "D0", "S0", "P002",
+    "R20", "R21", "P022", "R22", "R23", "X1", "Y1", "D1", "S1", "P102", "R30", "P122",
+    "R31", "R32", "R33", "X2", "Y2", "D2", "S2", "P202", "P222", "X3", "Y3", "D3",
+    "S3", "P302", "P32", "P33",
+)
+DIRECT = (0, 1, 2, 3, )
 
 
 def passed_along(value, axis, steps):
@@ -43,7 +54,8 @@
     n_seq, n_head, kv_heads, groups, reach,
     q_ref, k_ref, v_ref, w_ref, gain_ref, res_ref, out_ref,
     k_ext, v_ext, stage, w_all, ctx, acc, squares,
-    halo_send, halo_recv, pass_send, a_send, a_recv, a_local, c_send, c_recv, c_local, b_send, b_recv, relay_send, relay_recv,
+    halo_send, halo_recv, pass_send, a_send, a_recv, own_sem, c_send, c_recv,
+    unit_send, forward_send, relay_send, unit_recv,
     up_send, down_send, ctx_recv, sq_send, sq_recv,
 ):
     me = lax.axis_index("seq")
@@ -53,7 +65,13 @@
     feats = w_ref.shape[0]
     sub = n_seq // n_head
     span = reach * rows
-    sibling = me + 1 - 2 * lax.rem(me, 2)
+    core = lax.rem(me, 2)
+    chip = me // 2
+    even = core == 0
+    sibling = me + 1 - 2 * core
+    across = me + 2 - 4 * lax.rem(chip, 2)
+    along = me + 4 - 8 * (chip // 2)
+    corner = across + along - me
     pair = groups * size
 
     def remote(src, dst, send, recv, device):
@@ -61,6 +79,12 @@
             src_ref=src, dst_ref=dst, send_sem=send, recv_sem=recv,
             device_id=device, device_id_type=MESH,
         )
+
+    def order(s):
+        low = z < n_head // 2
+        near = jnp.where(low, z, n_head - 1 - z)
+        at = near if s == 0 else (1 - near if s == 1 else s)
+        return jnp.where(low, at, n_head - 1 - at)
 
     def halo(dist, g, kv, target):
         at = pl.ds(span - dist * rows, rows)
@@ -70,28 +94,6 @@
             src, dst = v_ref.at[g], v_ext.at[g, :, at]
         return remote(src, dst, halo_send.at[dist - 1, g, kv], halo_recv.at[dist - 1, g, kv], (target, z))
 
-    def piece(p, source, target):
-        return remote(
-            w_ref.at[:, pl.ds(pl.multiple_of(p * LANES, LANES), LANES)], stage.at[source],
-            a_send.at[p], a_recv.at[source], (target, z),
-        )
-
-    def own_piece():
-        return pltpu.make_async_copy(
-            w_ref.at[:, pl.ds(pl.multiple_of(me * LANES, LANES), LANES)], stage.at[me], a_local
-        )
-
-    def climb(h, source, target):
-        return remote(
-            stage.at[pl.ds(h * sub, sub)], w_all.at[me, source],
-            c_send.at[h], c_recv.at[source], (me, target),
-        )
-
-    def own_climb():
-        return pltpu.make_async_copy(stage.at[pl.ds(z * sub, sub)], w_all.at[me, z], c_local)
-
-    even = lax.rem(me, 2) == 0
-
     def passed_on(g, kv):
         near, far = pl.ds(span - rows, rows), pl.ds(span - 2 * rows, rows)
         if kv == 0:
@@ -111,23 +113,94 @@
             halo(2, g, 0, me + 2).start()
             halo(2, g, 1, me + 2).start()
 
-    start_halo(0)
-    own_piece().start()
-    for d in range(1, n_seq):
-        other = lax.rem(me + d, n_seq)
-        piece(other, me, other).start()
-
-    for g in range(1, kv_heads):
-        start_halo(g)
-
-    for dist in range(1, reach + 1):
-        @pl.when(me < dist)
-        def _():
-            at = pl.ds(span - dist * rows, rows)
-            k_ext[:, at, :] = jnp.zeros((kv_heads, rows, size), jnp.bfloat16)
-            v_ext[:, :, at] = jnp.zeros((kv_heads, size, rows), jnp.bfloat16)
-    k_ext[:, pl.ds(span, rows), :] = k_ref[...]
-    v_ext[:, :, pl.ds(span, rows)] = v_ref[...]
+    def columns(target):
+        return w_ref.at[:, pl.ds(pl.multiple_of(target * LANES, LANES), LANES)]
+
+    def piece(source, target, direct):
+        dst = w_all.at[target, z, lax.rem(source, sub)] if direct else stage.at[source]
+        return remote(columns(target), dst, a_send.at[target], a_recv.at[source], (target, z))
+
+    def scatter(target):
+        @pl.when(me // sub == z)
+        def _():
+            piece(me, target, True).start()
+
+        @pl.when(me // sub != z)
+        def _():
+            piece(me, target, False).start()
+
+    def own_copy():
+        return pltpu.make_async_copy(columns(me), w_all.at[me, z, lax.rem(me, sub)], own_sem)
+
+    def own_climb():
+        return remote(
+            columns(me), w_all.at[me, z, lax.rem(me, sub)],
+            c_send.at[me], c_recv.at[z, lax.rem(me, sub)], (me, me // sub),
+        )
+
+    def climb(source):
+        return remote(
+            stage.at[source], w_all.at[me, z, lax.rem(source, sub)],
+            c_send.at[source], c_recv.at[z, lax.rem(source, sub)], (me, source // sub),
+        )
+
+    def take_piece(source):
+        piece(source, me, False).wait_recv()
+
+        @pl.when(source // sub != z)
+        def _():
+            climb(source).start()
+
+    others = (across, along, across + 1 - 2 * core, along + 1 - 2 * core, corner, corner + 1 - 2 * core, sibling)
+
+    def unit(owner, r, send, target):
+        return remote(w_all.at[owner, r], w_all.at[owner, r], send, unit_recv.at[owner, r], (target, z))
+
+    def send_unit(s):
+        r = order(s)
+        if s == 0:
+            @pl.when(me // sub == z)
+            def _():
+                own_copy().wait()
+
+        else:
+            for j in range(sub):
+                remote(stage.at[0], w_all.at[me, r, j], c_send.at[0], c_recv.at[r, j], (me, r)).wait_recv()
+        unit(me, r, unit_send.at[0, s], across).start()
+        unit(me, r, unit_send.at[1, s], along).start()
+        if s in DIRECT:
+            unit(me, r, forward_send.at[s], corner).start()
+        unit(me, r, relay_send.at[0, s], sibling).start()
+
+    def take_across(s):
+        r = order(s)
+        unit(across, r, unit_send.at[0, s], me).wait_recv()
+
+        @pl.when(jnp.logical_and(even, s not in DIRECT))
+        def _():
+            unit(across, r, forward_send.at[s], along).start()
+
+        unit(across, r, relay_send.at[1, s], sibling).start()
+
+    def take_along(s):
+        r = order(s)
+        unit(along, r, unit_send.at[0, s], me).wait_recv()
+
+        @pl.when(jnp.logical_and(jnp.logical_not(even), s not in DIRECT))
+        def _():
+            unit(along, r, forward_send.at[s], across).start()
+
+        unit(along, r, relay_send.at[2, s], sibling).start()
+
+    def take_corner(s):
+        r = order(s)
+        unit(corner, r, unit_send.at[0, s], me).wait_recv()
+        unit(corner, r, relay_send.at[3, s], sibling).start()
+
+    def take_relayed(s):
+        r = order(s)
+        for owner in (me, across, along, corner):
+            unit(owner + 1 - 2 * core, r, unit_send.at[0, s], me).wait_recv()
 
     def chunk(r, g):
         return ctx.at[r, pl.ds(g * pair, pair), :]
@@ -138,53 +211,26 @@
     def ctx_down(r, g):
         return remote(chunk(r, g), chunk(r, g), down_send.at[r, g], ctx_recv.at[r, g], (me, z - 1))
 
-    def arrive(dist, g, then_send):
-        @pl.when(z - dist >= 0)
-        def _():
-            r = z - dist
+    inner = jnp.logical_and(z >= 1, z + 1 < n_head)
+
+    def arrive(s, g):
+        r = order(s)
+
+        @pl.when(inner)
+        def _():
             ctx_up(r, g).wait_recv()
-            if then_send:
-                @pl.when(z + 1 < n_head)
-                def _():
-                    ctx_up(r, g).start()
-
-        @pl.when(z + dist < n_head)
-        def _():
-            r = z + dist
-            ctx_down(r, g).wait_recv()
-            if then_send:
-                @pl.when(z - 1 >= 0)
-                def _():
-                    ctx_down(r, g).start()
-
-    offsets = n_seq // 2
-
-    def spread(m, source, target):
-        return remote(w_all.at[source], w_all.at[source], b_send.at[m], b_recv.at[m], (target, z))
-
-    def relay(m, source):
-        return remote(w_all.at[source], w_all.at[source], relay_send.at[m], relay_recv.at[m], (sibling, z))
-
-    def start_climb():
-        own_piece().wait()
-        for d in range(1, n_seq):
-            source = lax.rem(me - d + n_seq, n_seq)
-            piece(source, source, me).wait_recv()
-        own_climb().start()
-        for d in range(1, n_head):
-            h = lax.rem(z + d, n_head)
-            climb(h, z, h).start()
-
-    def start_spread():
-        own_climb().wait()
-        for d in range(1, n_head):
-            climb(0, lax.rem(z + d, n_head), z).wait_recv()
-        for m in range(1, offsets):
-            spread(m, me, lax.rem(me + 2 * m, n_seq)).start()
-        relay(0, me).start()
+
+        @pl.when(jnp.logical_and(inner, r < z))
+        def _():
+            ctx_up(r, g).start()
+
+        @pl.when(jnp.logical_and(inner, r > z))
+        def _():
+            ctx_down(r, g).start()
 
     blocks = span // TILE + 1
-    for g in range(kv_heads):
+
+    def attend(g):
         for dist in range(1, reach + 1):
             @pl.when(me >= dist)
             def _():
@@ -242,46 +288,66 @@
         @pl.when(z >= 1)
         def _():
             ctx_down(z, g).start()
-        if g == 0:
-            start_climb()
-        if g >= 1:
-            arrive(1, g - 1, True)
-    start_spread()
-
-    arrive(1, kv_heads - 1, True)
-    for dist in range(2, n_head):
-        for g in range(kv_heads):
-            arrive(dist, g, dist + 1 < n_head)
 
     tile = next(t for t in range(256, 0, -16) if feats % t == 0)
 
-    def project(p, init):
-        block = jnp.concatenate(
-            [ctx[r, pl.ds(pl.multiple_of(p * LANES, LANES), LANES), :] for r in range(n_head)], 0
-        )
+    def project(s, g, n=1):
+        r = order(s)
+        if s > 0:
+            @pl.when(jnp.logical_not(inner))
+            def _():
+                for i in range(n):
+                    ctx_up(r, g + i).wait_recv()
+
+        block = ctx[r, pl.ds(g * pair, n * pair), :]
         for j in range(sub):
             @pl.loop(0, feats // tile)
             def _(t):
                 at = pl.ds(pl.multiple_of(t * tile, tile), tile)
-                w = jnp.concatenate([w_all[p, r, j, at, :] for r in range(n_head)], 1)
+                w = jnp.concatenate([w_all[g * groups + i, r, j, at, :] for i in range(n * groups)], 1)
                 got = jnp.dot(w, block, preferred_element_type=jnp.float32)
-                if init:
+                if s == 0 and g == 0:
                     acc[j, at, :] = got
                 else:
                     acc[j, at, :] += got
 
-    project(me, True)
-    relay(0, sibling).wait_recv()
-    project(sibling, False)
-    for m in range(1, offsets):
-        source = lax.rem(me - 2 * m + n_seq, n_seq)
-        spread(m, source, me).wait_recv()
-        relay(m, source).start()
-        project(source, False)
-    for m in range(1, offsets):
-        source = lax.rem(sibling - 2 * m + n_seq, n_seq)
-        relay(m, source).wait_recv()
-        project(source, False)
+    barrier = pltpu.get_barrier_semaphore()
+    for d in range(1, n_seq):
+        pl.semaphore_signal(barrier, inc=1, device_id=(lax.rem(me + d, n_seq), z), device_id_type=MESH)
+    for d in range(1, n_head):
+        pl.semaphore_signal(barrier, inc=1, device_id=(me, lax.rem(z + d, n_head)), device_id_type=MESH)
+    pl.semaphore_wait(barrier, n_seq + n_head - 2)
+
+    @pl.when(me // sub == z)
+    def _():
+        own_copy().start()
+
+    @pl.when(me // sub != z)
+    def _():
+        own_climb().start()
+
+    for word in LAUNCH:
+        if word[0] == "H":
+            start_halo(int(word[1]))
+        else:
+            scatter(others[int(word[1])])
+
+    for dist in range(1, reach + 1):
+        @pl.when(me < dist)
+        def _():
+            at = pl.ds(span - dist * rows, rows)
+            k_ext[:, at, :] = jnp.zeros((kv_heads, rows, size), jnp.bfloat16)
+            v_ext[:, :, at] = jnp.zeros((kv_heads, size, rows), jnp.bfloat16)
+    k_ext[:, pl.ds(span, rows), :] = k_ref[...]
+    v_ext[:, :, pl.ds(span, rows)] = v_ref[...]
+
+    def take(n):
+        take_piece(others[n])
+
+    steps = {"T": take, "A": attend, "C": send_unit, "X": take_across, "Y": take_along, "D": take_corner,
+             "S": take_relayed, "R": arrive, "P": project}
+    for word in PLAN:
+        steps[word[0]](*[int(c) for c in word[1:]])
 
     mine = jnp.zeros((8, rows), jnp.float32)
     for j in range(sub):
@@ -321,33 +387,43 @@
         def _():
             passed_on(g, 0).wait_send()
             passed_on(g, 1).wait_send()
-    for d in range(1, n_seq):
-        piece(lax.rem(me + d, n_seq), me, me).wait_send()
-    for d in range(1, n_head):
-        climb(lax.rem(z + d, n_head), z, z).wait_send()
-    for m in range(1, offsets):
-        spread(m, me, me).wait_send()
-        relay(m, lax.rem(me - 2 * m + n_seq, n_seq)).wait_send()
-    relay(0, me).wait_send()
+    for target in others:
+        piece(me, target, False).wait_send()
+        source = target
+
+        @pl.when(source // sub != z)
+        def _():
+            climb(source).wait_send()
+
+    @pl.when(me // sub != z)
+    def _():
+        own_climb().wait_send()
+    for s in range(n_head):
+        for way in range(2):
+            unit(me, s, unit_send.at[way, s], me).wait_send()
+        unit(me, s, forward_send.at[s], me).wait_send()
+        for way in range(4):
+            unit(me, s, relay_send.at[way, s], me).wait_send()
     for g in range(kv_heads):
-        for dist in range(n_head - 1):
-            @pl.when(jnp.logical_and(z - dist >= 0, z + 1 < n_head))
+        for r in range(n_head):
+            @pl.when(jnp.logical_and(r <= z, z + 1 < n_head))
             def _():
-                ctx_up(z - dist, g).wait_send()
-
-            @pl.when(jnp.logical_and(z + dist < n_head, z >= 1))
+                ctx_up(r, g).wait_send()
+
+            @pl.when(jnp.logical_and(r >= z, z >= 1))
             def _():
-                ctx_down(z + dist, g).wait_send()
-
-
-def fits(rows, heads_rows, kv_heads, feats, n_seq, n_head):
+                ctx_down(r, g).wait_send()
+
+
+def fits(rows, heads_rows, kv_heads, groups, feats, n_seq, n_head):
     return (
-        n_seq % 2 == 0
-        and n_seq % n_head == 0
+        n_seq == 8
+        and n_head in (2, 4)
+        and groups == 2
         and heads_rows == n_seq * LANES
         and rows % TILE == 0
         and VISIBLE_SPAN == 2 * rows
-        and kv_heads >= 2
+        and kv_heads * groups == n_seq
         and feats % 16 == 0
     )
 
@@ -380,12 +456,12 @@
             pltpu.VMEM((sub, feats, rows), f32),
             pltpu.VMEM((n_head, 8, rows), f32),
             dma((reach, kv_heads, 2)), dma((reach, kv_heads, 2)), dma((kv_heads, 2)),
-            dma((n_seq,)), dma((n_seq,)), dma, dma((n_head,)), dma((n_head,)), dma,
-            dma((n_seq // 2,)), dma((n_seq // 2,)), dma((n_seq // 2,)), dma((n_seq // 2,)),
+            dma((n_seq,)), dma((n_seq,)), dma, dma((n_seq,)), dma((n_head, sub)),
+            dma((2, n_head)), dma((n_head,)), dma((4, n_head)), dma((n_seq, n_head)),
             dma((n_head, kv_heads)), dma((n_head, kv_heads)), dma((n_head, kv_heads)),
             dma((n_head,)), dma((n_head,)),
         ],
-        compiler_params=pltpu.CompilerParams(has_side_effects=True, vmem_limit_bytes=60 * 1024 * 1024),
+        compiler_params=pltpu.CompilerParams(has_side_effects=True, collective_id=0, vmem_limit_bytes=60 * 1024 * 1024),
     )(q, k, v, out_weight.T, post_gain[:, None], residual.T)
     return out.T
 
@@ -434,7 +510,7 @@
 def on_device(positions, queries, keys, values, out_weight, post_gain, residual):
     n_seq, n_head = lax.axis_size("seq"), lax.axis_size("head")
     rows, kv_heads, _ = keys.shape
-    body = fused if fits(rows, out_weight.shape[0], kv_heads, out_weight.shape[1], n_seq, n_head) else general
+    body = fused if fits(rows, out_weight.shape[0], kv_heads, queries.shape[1] // kv_heads, out_weight.shape[1], n_seq, n_head) else general
     return body(positions, queries, keys, values, out_weight, post_gain, residual)
 
 

time: 165 us -> 133 us (0.81)
  Pallas kernels: 154 us -> 121 us
    pallas_call x1, Pallas kernels: 154 us -> 121 us  [fused(): pl.pallas_call(functools.partial(layer_kernel, n_seq, n_head, kv_heads, g...]
where the time goes in v1:
time: 133 us
  Pallas kernels  121 us (91%)
  other arithmetic  6.6 us (5%)
  local copies, waits for them, and re-layouts  4.78 us (4%)
    pallas_call x1, Pallas kernels, fused(): pl.pallas_call(functools.partial(layer_kernel, n_seq, n_head, kv_heads, g...  121 us
    unnamed x12, local copies, waits for them, and re-layouts  3.67 us

profile of v1, /device:TPU:0, one launch (start us, length us, event | category | flops | bytes accessed | tf_op | source)
XLA Modules:
  0.0 132.7 jit_solution(17265563594970467918)
XLA Ops:
  0.0 1.4 %copy_convert_fusion = f32[512,8,128]{2,0,1:T(8,128)S(1)} fusion(bf16[512,8,128]{2,1,0:T(8,128)(2,1)} %param.8), kind=kLoop, calls=%fused_computation.9 | loop fusion | flops 524288 | bytes 3145728 | tf_op jit(solution)/shard_map/convert_element_type | solution.py:48
  1.4 0.0 copy-start.4
  1.4 0.7 slice_negate_fusion
  2.1 0.0 copy-start
  2.1 0.0 copy-done.4
  2.1 1.0 multiply_cosine_fusion
  3.1 0.2 pad_maximum_fusion
  3.3 0.0 copy-done
  3.3 0.0 copy-start.1
  3.4 1.7 %fusion.2.q_ref = bf16[8,512,128]{2,1,0:T(8,128)(2,1)} fusion(f32[512,8,64]{2,0,1:T(8,128)S(1)} %get-tuple-element.6, f32[512,8,64]{2,0,1:T(8,128)S(1)} %get-tuple-element.5, f32[512,128]{1,0:T(8,128)S(1)} %get-tuple-element.12, f32[512,128]{1,0:T(8,128)S(1)} %get-tuple-element.11, bf16[512,8,128]{2,1,0:T(8,128)(2,1)S(1)} %copy-done), kind=kLoop, calls=%fused_computation.4 | loop fusion | flops 3145728 | bytes 4718592 | tf_op jit(solution)/shard_map/transpose | solution.py:439
  5.1 0.0 copy-done.1
  5.1 0.1 copy_convert_fusion.1
  5.1 0.3 slice_negate_fusion.1
  5.5 0.0 copy-start.2
  5.5 0.0 copy-start.3
  5.5 1.2 fusion.5.k_ref
  6.7 0.0 copy-done.2
  6.7 1.1 copy.13
  7.9 0.0 copy-done.3
  7.9 1.1 broadcast_in_dim.3.gain_ref
  9.0 121.2 %shard_map.73 = bf16[1344,512]{1,0:T(8,128)(2,1)} custom-call(bf16[8,512,128]{2,1,0:T(8,128)(2,1)} %fusion.2.q_ref, bf16[4,512,128]{2,1,0:T(8,128)(2,1)} %fusion.5.k_ref, bf16[4,128,512]{2,1,0:T(8,128)(2,1)} %bitcast.9, bf16[672,1024]{1,0:T(8,128)(2,1)} %bitcast.10, f32[1344,1]{1,0:T(8,128)} %broadcast_in_dim.3.gain_ref, bf16[1344,512]{1,0:T(8,128)(2,1)} %bitcast.11), custom_call_target="tpu_custom_call" | custom-call | tf_op jit(solution)/shard_map/pallas_call | solution.py:445
  130.1 2.5 %copy.22 = bf16[512,1344]{0,1:T(8,128)(2,1)} copy(bf16[512,1344]{0,1:T(8,128)(2,1)} %bitcast.8) | data formatting | bytes 2752512
  (2 shorter events, 0.0 us)
Async XLA Ops:
  1.4 0.8 copy-start.4
  2.1 1.2 copy-start
  3.3 1.7 %copy-start.1 = (bf16[512,4,128]{2,1,0:T(4,128)(2,1)S(1)}, bf16[512,4,128]{2,1,0:T(4,128)(2,1)}, u32[]{:S(2)}) copy-start(bf16[512,4,128]{2,1,0:T(4,128)(2,1)} %param.9) | copy-start | bytes 1572868
  5.5 1.2 copy-start.2
  5.5 2.4 %copy-start.3 = (f32[1344]{0:T(1024)S(1)}, f32[1344]{0:T(1024)}, u32[]{:S(2)}) copy-start(f32[1344]{0:T(1024)} %param.12) | copy-start | bytes 16132

commit v2 on v1

--- a/solution.py
+++ b/solution.py
@@ -21,13 +21,13 @@
 LANES = 128
 MESH = pl.DeviceIdType.MESH
 LAUNCH = (
-    "Z0", "Z1", "Z2", "Z3", "Z4", "Z5", "Z6", "H0", "H1", "H2", "H3",
+    "Z0", "Z2", "Z3", "Z4", "Z5", "Z6", "H0", "H1", "H2", "H3", "Z1",
 )
 PLAN = (
     "T6", "T0", "T1", "T2", "T3", "T4", "T5", "C0", "A0", "A1", "C1", "A2",
     "A3", "C2", "C3", "R10", "R11", "R12", "R13", "X0", "Y0", "D0", "S0", "P002",
-    "R20", "R21", "P022", "R22", "R23", "X1", "Y1", "D1", "S1", "P102", "R30", "P122",
-    "R31", "R32", "R33", "X2", "Y2", "D2", "S2", "P202", "P222", "X3", "Y3", "D3",
+    "R20", "R21", "P022", "R22", "R23", "R31", "X1", "Y1", "D1", "S1", "P102", "R30",
+    "P122", "R32", "R33", "X2", "Y2", "D2", "S2", "P202", "P222", "X3", "Y3", "D3",
     "S3", "P302", "P32", "P33",
 )
 DIRECT = (0, 1, 2, 3, )
@@ -52,16 +52,17 @@
 
 def layer_kernel(
     n_seq, n_head, kv_heads, groups, reach,
-    q_ref, k_ref, v_ref, w_ref, gain_ref, res_ref, out_ref,
-    k_ext, v_ext, stage, w_all, ctx, acc, squares,
+    q_hbm, k_hbm, v_hbm, cos_hbm, sin_hbm, w_hbm, gain_hbm, res_hbm, out_ref,
+    q_raw, k_raw, v_raw, cos_ref, sin_ref, w_ref, gain_ref, res_ref, load_sem,
+    q_ref, gain_col, k_ext, v_ext, stage, w_all, ctx, acc, squares,
     halo_send, halo_recv, pass_send, a_send, a_recv, own_sem, c_send, c_recv,
     unit_send, forward_send, relay_send, unit_recv,
     up_send, down_send, ctx_recv, sq_send, sq_recv,
 ):
     me = lax.axis_index("seq")
     z = lax.axis_index("head")
-    rows = k_ref.shape[1]
-    size = k_ref.shape[2]
+    rows = k_raw.shape[0]
+    size = k_raw.shape[2]
     feats = w_ref.shape[0]
     sub = n_seq // n_head
     span = reach * rows
@@ -87,11 +88,11 @@
         return jnp.where(low, at, n_head - 1 - at)
 
     def halo(dist, g, kv, target):
-        at = pl.ds(span - dist * rows, rows)
+        at, own = pl.ds(span - dist * rows, rows), pl.ds(span, rows)
         if kv == 0:
-            src, dst = k_ref.at[g], k_ext.at[g, at, :]
+            src, dst = k_ext.at[g, own, :], k_ext.at[g, at, :]
         else:
-            src, dst = v_ref.at[g], v_ext.at[g, :, at]
+            src, dst = v_ext.at[g, :, own], v_ext.at[g, :, at]
         return remote(src, dst, halo_send.at[dist - 1, g, kv], halo_recv.at[dist - 1, g, kv], (target, z))
 
     def passed_on(g, kv):
@@ -311,11 +312,31 @@
                 else:
                     acc[j, at, :] += got
 
+    loads = [pltpu.make_async_copy(src, dst, load_sem.at[i]) for i, (src, dst) in enumerate((
+        (k_hbm, k_raw), (v_hbm, v_raw), (cos_hbm, cos_ref), (sin_hbm, sin_ref),
+        (w_hbm, w_ref), (q_hbm, q_raw), (gain_hbm, gain_ref), (res_hbm, res_ref),
+    ))]
     barrier = pltpu.get_barrier_semaphore()
     for d in range(1, n_seq):
         pl.semaphore_signal(barrier, inc=1, device_id=(lax.rem(me + d, n_seq), z), device_id_type=MESH)
     for d in range(1, n_head):
         pl.semaphore_signal(barrier, inc=1, device_id=(me, lax.rem(z + d, n_head)), device_id_type=MESH)
+    for load in loads:
+        load.start()
+
+    def turned(x):
+        x = jnp.swapaxes(x.astype(jnp.float32), 0, 1)
+        return (x * cosine[None] + pltpu.roll(x, size // 2, 2) * sine[None]).astype(jnp.bfloat16)
+
+    part = rows // 4
+    for load in loads[:4]:
+        load.wait()
+    for t in range(0, rows, part):
+        cosine, sine = cos_ref[t : t + part, :], sin_ref[t : t + part, :]
+        k_ext[:, span + t : span + t + part, :] = turned(k_raw[t : t + part])
+    for g in range(kv_heads):
+        v_ext[g, :, span : span + rows] = v_raw[:, g, :].T
+    loads[4].wait()
     pl.semaphore_wait(barrier, n_seq + n_head - 2)
 
     @pl.when(me // sub == z)
@@ -332,14 +353,20 @@
         else:
             scatter(others[int(word[1])])
 
+    loads[5].wait()
+    for t in range(0, rows, part):
+        cosine, sine = cos_ref[t : t + part, :], sin_ref[t : t + part, :]
+        q_ref[:, t : t + part, :] = turned(q_raw[t : t + part])
     for dist in range(1, reach + 1):
         @pl.when(me < dist)
         def _():
             at = pl.ds(span - dist * rows, rows)
             k_ext[:, at, :] = jnp.zeros((kv_heads, rows, size), jnp.bfloat16)
             v_ext[:, :, at] = jnp.zeros((kv_heads, size, rows), jnp.bfloat16)
-    k_ext[:, pl.ds(span, rows), :] = k_ref[...]
-    v_ext[:, :, pl.ds(span, rows)] = v_ref[...]
+    loads[6].wait()
+    for first in range(0, gain_ref.shape[1], LANES):
+        count = min(LANES, gain_ref.shape[1] - first)
+        gain_col[first : first + count, :] = jnp.broadcast_to(gain_ref[:, first : first + count], (LANES, count)).T
 
     def take(n):
         take_piece(others[n])
@@ -362,12 +389,14 @@
         sq(d, lax.rem(z + d, n_head)).start()
     for d in range(1, n_head):
         sq(d, z).wait_recv()
+    loads[7].wait()
     whole = jnp.sum(jnp.sum(squares[...], axis=0), axis=0, keepdims=True)
     inverse = lax.rsqrt(whole / (n_head * sub * feats) + EPS)
     for j in range(sub):
         at = pl.ds(j * feats, feats)
+        gain = jnp.concatenate([gain_col[at, :]] * (rows // LANES), 1)
         out_ref[at, :] = (
-            res_ref[at, :].astype(jnp.float32) + gain_ref[at, :] * (acc[j] * inverse)
+            res_ref[at, :].astype(jnp.float32) + gain * (acc[j] * inverse)
         ).astype(jnp.bfloat16)
 
     for d in range(1, n_head):
@@ -436,18 +465,25 @@
     width = residual.shape[1]
     sub = n_seq // n_head
     reach = VISIBLE_SPAN // rows
-    q = rotate(queries, positions).transpose(1, 0, 2)
-    k = rotate(keys, positions).transpose(1, 0, 2)
-    v = values.transpose(1, 2, 0)
+    half = size // 2
+    inverse = 10000.0 ** (-2.0 * jnp.arange(half, dtype=jnp.float32) / size)
+    angle = positions.astype(jnp.float32)[:, None] * inverse[None, :]
+    cosine = jnp.concatenate([jnp.cos(angle), jnp.cos(angle)], -1)
+    sine = jnp.concatenate([-jnp.sin(angle), jnp.sin(angle)], -1)
     bf16, f32 = jnp.bfloat16, jnp.float32
     dma = pltpu.SemaphoreType.DMA
     spec = pl.BlockSpec(memory_space=pltpu.VMEM)
     out = pl.pallas_call(
         functools.partial(layer_kernel, n_seq, n_head, kv_heads, groups, reach),
         out_shape=jax.ShapeDtypeStruct((width, rows), bf16),
-        in_specs=[spec] * 6,
+        in_specs=[pl.BlockSpec(memory_space=pl.ANY)] * 8,
         out_specs=spec,
         scratch_shapes=[
+            pltpu.VMEM(queries.shape, bf16), pltpu.VMEM(keys.shape, bf16), pltpu.VMEM(keys.shape, bf16),
+            pltpu.VMEM((rows, size), f32), pltpu.VMEM((rows, size), f32), pltpu.VMEM(out_weight.shape[::-1], bf16),
+            pltpu.VMEM((1, width), f32), pltpu.VMEM((width, rows), bf16), dma((8,)),
+            pltpu.VMEM((kv_heads * groups, rows, size), bf16),
+            pltpu.VMEM((width, LANES), f32),
             pltpu.VMEM((kv_heads, (reach + 1) * rows, size), bf16),
             pltpu.VMEM((kv_heads, size, (reach + 1) * rows), bf16),
             pltpu.VMEM((n_seq, feats, LANES), bf16),
@@ -461,8 +497,8 @@
             dma((n_head, kv_heads)), dma((n_head, kv_heads)), dma((n_head, kv_heads)),
             dma((n_head,)), dma((n_head,)),
         ],
-        compiler_params=pltpu.CompilerParams(has_side_effects=True, collective_id=0, vmem_limit_bytes=60 * 1024 * 1024),
-    )(q, k, v, out_weight.T, post_gain[:, None], residual.T)
+        compiler_params=pltpu.CompilerParams(has_side_effects=True, collective_id=0, vmem_limit_bytes=44 * 1024 * 1024),
+    )(queries, keys, values, cosine, sine, out_weight.T, post_gain[None, :], residual.T)
     return out.T
 
 

time: 133 us -> 126 us (0.947)
  other arithmetic: 6.6 us -> 2.03 us
  Pallas kernels: 121 us -> 118 us
    pallas_call x1, Pallas kernels: 121 us -> 118 us  [fused(): pl.pallas_call(functools.partial(layer_kernel, n_seq, n_head, kv_heads, g...]
    transpose x2 -> x0, other arithmetic: 2.93 us -> none  [the longest x1 1.7 us: fused(): q = rotate(queries, positions).transpose(1, 0, 2)]
    unnamed x12 -> x11, local copies, waits for them, and re-layouts: 3.67 us -> 4.69 us
where the time goes in v2:
time: 126 us
  Pallas kernels  118 us (94%)
  local copies, waits for them, and re-layouts  5.39 us (4%)
  other arithmetic  2.03 us (2%)
    pallas_call x1, Pallas kernels, fused(): pl.pallas_call(functools.partial(layer_kernel, n_seq, n_head, kv_heads, g...  118 us
    unnamed x11, local copies, waits for them, and re-layouts  4.69 us

profile of v2, /device:TPU:0, one launch (start us, length us, event | category | flops | bytes accessed | tf_op | source)
XLA Modules:
  0.0 125.6 jit_solution(750025553242294851)
XLA Ops:
  0.0 0.0 copy-start
  0.0 0.0 copy-start.3
  0.0 0.8 convert_element_type.3
  0.8 0.7 broadcast_in_dim.2.gain_hbm
  1.5 1.0 fusion
  2.5 0.2 pad_maximum_fusion
  2.7 0.0 copy-done
  2.8 0.0 copy-done.3
  2.8 0.0 copy-start.1
  2.8 1.3 %copy-done.1 = bf16[512,1344]{0,1:T(8,128)(2,1)S(1)} copy-done((bf16[512,1344]{0,1:T(8,128)(2,1)S(1)}, bf16[512,1344]{0,1:T(8,128)(2,1)}, u32[]{:S(2)}) %copy-start.1) | copy-done | bytes 1376280
  4.1 0.0 copy-start.2
  4.1 1.2 copy-done.2
  5.3 0.0 copy-start.4
  5.3 1.0 copy-done.4
  6.4 118.1 %shard_map.73 = bf16[1344,512]{1,0:T(8,128)(2,1)S(1)} custom-call(bf16[512,8,128]{2,1,0:T(8,128)(2,1)S(1)} %copy-done.2, bf16[512,4,128]{2,1,0:T(4,128)(2,1)S(1)} %copy-done.3, bf16[512,4,128]{2,1,0:T(4,128)(2,1)S(1)} %copy-done.4, f32[512,128]{1,0:T(8,128)S(1)} %get-tuple-element.8.cos_hbm, f32[512,128]{1,0:T(8,128)S(1)} %get-tuple-element.9.sin_hbm, ...), custom_call_target="tpu_custom_call" | custom-call | tf_op jit(solution)/shard_map/pallas_call | solution.py:476
  124.5 1.1 copy.9
  (1 shorter events, 0.0 us)
Async XLA Ops:
  0.0 2.7 %copy-start = (bf16[1024,672]{0,1:T(8,128)(2,1)S(1)}, bf16[1024,672]{0,1:T(8,128)(2,1)}, u32[]{:S(2)}) copy-start(bf16[1024,672]{0,1:T(8,128)(2,1)} %param.11) | copy-start | bytes 4128772
  0.0 2.8 %copy-start.3 = (bf16[512,4,128]{2,1,0:T(4,128)(2,1)S(1)}, bf16[512,4,128]{2,1,0:T(4,128)(2,1)}, u32[]{:S(2)}) copy-start(bf16[512,4,128]{2,1,0:T(4,128)(2,1)} %k_hbm.1) | copy-start | bytes 1572868
  2.8 1.3 %copy-start.1 = (bf16[512,1344]{0,1:T(8,128)(2,1)S(1)}, bf16[512,1344]{0,1:T(8,128)(2,1)}, u32[]{:S(2)}) copy-start(bf16[512,1344]{0,1:T(8,128)(2,1)} %param.13) | copy-start | bytes 4128772
  4.1 1.2 copy-start.2
  5.3 1.0 copy-start.4

commit v3 on v2

--- a/solution.py
+++ b/solution.py
@@ -21,11 +21,11 @@
 LANES = 128
 MESH = pl.DeviceIdType.MESH
 LAUNCH = (
-    "Z0", "Z2", "Z3", "Z4", "Z5", "Z6", "H0", "H1", "H2", "H3", "Z1",
+    "Z4", "Z0", "Z1", "Z5", "Z2", "Z3", "Z6", "H0", "H1", "H2", "H3",
 )
 PLAN = (
-    "T6", "T0", "T1", "T2", "T3", "T4", "T5", "C0", "A0", "A1", "C1", "A2",
-    "A3", "C2", "C3", "R10", "R11", "R12", "R13", "X0", "Y0", "D0", "S0", "P002",
+    "T6", "T4", "T0", "T1", "T5", "T2", "T3", "C0", "A0", "A1", "A2", "A3",
+    "C1", "C2", "C3", "R10", "R11", "R12", "R13", "X0", "Y0", "D0", "S0", "P002",
     "R20", "R21", "P022", "R22", "R23", "R31", "X1", "Y1", "D1", "S1", "P102", "R30",
     "P122", "R32", "R33", "X2", "Y2", "D2", "S2", "P202", "P222", "X3", "Y3", "D3",
     "S3", "P302", "P32", "P33",
@@ -52,8 +52,9 @@
 
 def layer_kernel(
     n_seq, n_head, kv_heads, groups, reach,
-    q_hbm, k_hbm, v_hbm, cos_hbm, sin_hbm, w_hbm, gain_hbm, res_hbm, out_ref,
-    q_raw, k_raw, v_raw, cos_ref, sin_ref, w_ref, gain_ref, res_ref, load_sem,
+    q_hbm, k_hbm, v_hbm, pos_hbm, rate_hbm, w_hbm, gain_hbm, res_hbm, out_ref,
+    q_raw, k_raw, v_raw, pos_ref, rate_ref, w_ref, gain_ref, res_ref, load_sem,
+    cos_ref, sin_ref,
     q_ref, gain_col, k_ext, v_ext, stage, w_all, ctx, acc, squares,
     halo_send, halo_recv, pass_send, a_send, a_recv, own_sem, c_send, c_recv,
     unit_send, forward_send, relay_send, unit_recv,
@@ -293,6 +294,7 @@
     tile = next(t for t in range(256, 0, -16) if feats % t == 0)
 
     def project(s, g, n=1):
+        last = s == n_head - 1 and g + n == kv_heads
         r = order(s)
         if s > 0:
             @pl.when(jnp.logical_not(inner))
@@ -307,13 +309,14 @@
                 at = pl.ds(pl.multiple_of(t * tile, tile), tile)
                 w = jnp.concatenate([w_all[g * groups + i, r, j, at, :] for i in range(n * groups)], 1)
                 got = jnp.dot(w, block, preferred_element_type=jnp.float32)
-                if s == 0 and g == 0:
-                    acc[j, at, :] = got
-                else:
-                    acc[j, at, :] += got
+                if s > 0 or g > 0:
+                    got = got + acc[j, at, :]
+                acc[j, at, :] = got
+                if last:
+                    squares[0] += jnp.sum((got * got).reshape(tile // 8, 8, rows), axis=0)
 
     loads = [pltpu.make_async_copy(src, dst, load_sem.at[i]) for i, (src, dst) in enumerate((
-        (k_hbm, k_raw), (v_hbm, v_raw), (cos_hbm, cos_ref), (sin_hbm, sin_ref),
+        (pos_hbm, pos_ref), (rate_hbm, rate_ref), (k_hbm, k_raw), (v_hbm, v_raw),
         (w_hbm, w_ref), (q_hbm, q_raw), (gain_hbm, gain_ref), (res_hbm, res_ref),
     ))]
     barrier = pltpu.get_barrier_semaphore()
@@ -329,7 +332,16 @@
         return (x * cosine[None] + pltpu.roll(x, size // 2, 2) * sine[None]).astype(jnp.bfloat16)
 
     part = rows // 4
-    for load in loads[:4]:
+    for load in loads[:2]:
+        load.wait()
+    tokens = pos_ref[...].reshape(1, rows).astype(jnp.float32)
+    early = lax.broadcasted_iota(jnp.int32, (size, size), 1) < size // 2
+    for t in range(0, rows, size):
+        angle = jnp.broadcast_to(tokens[:, t : t + size], (size, size)).T * rate_ref[...]
+        cos_ref[t : t + size, :] = jnp.cos(angle)
+        sine = jnp.sin(angle)
+        sin_ref[t : t + size, :] = jnp.where(early, -sine, sine)
+    for load in loads[2:4]:
         load.wait()
     for t in range(0, rows, part):
         cosine, sine = cos_ref[t : t + part, :], sin_ref[t : t + part, :]
@@ -353,6 +365,7 @@
         else:
             scatter(others[int(word[1])])
 
+    squares[0] = jnp.zeros((8, rows), jnp.float32)
     loads[5].wait()
     for t in range(0, rows, part):
         cosine, sine = cos_ref[t : t + part, :], sin_ref[t : t + part, :]
@@ -364,9 +377,10 @@
             k_ext[:, at, :] = jnp.zeros((kv_heads, rows, size), jnp.bfloat16)
             v_ext[:, :, at] = jnp.zeros((kv_heads, size, rows), jnp.bfloat16)
     loads[6].wait()
-    for first in range(0, gain_ref.shape[1], LANES):
-        count = min(LANES, gain_ref.shape[1] - first)
-        gain_col[first : first + count, :] = jnp.broadcast_to(gain_ref[:, first : first + count], (LANES, count)).T
+    gain_row = gain_ref[...].reshape(1, gain_ref.shape[0])
+    for first in range(0, gain_ref.shape[0], LANES):
+        count = min(LANES, gain_ref.shape[0] - first)
+        gain_col[first : first + count, :] = jnp.broadcast_to(gain_row[:, first : first + count], (LANES, count)).T
 
     def take(n):
         take_piece(others[n])
@@ -375,12 +389,6 @@
              "S": take_relayed, "R": arrive, "P": project}
     for word in PLAN:
         steps[word[0]](*[int(c) for c in word[1:]])
-
-    mine = jnp.zeros((8, rows), jnp.float32)
-    for j in range(sub):
-        value = acc[j]
-        mine = mine + jnp.sum((value * value).reshape(feats // 8, 8, rows), axis=0)
-    squares[0] = mine
 
     def sq(d, target):
         return remote(squares.at[0], squares.at[d], sq_send.at[d - 1], sq_recv.at[d - 1], (me, target))
@@ -467,21 +475,20 @@
     reach = VISIBLE_SPAN // rows
     half = size // 2
     inverse = 10000.0 ** (-2.0 * jnp.arange(half, dtype=jnp.float32) / size)
-    angle = positions.astype(jnp.float32)[:, None] * inverse[None, :]
-    cosine = jnp.concatenate([jnp.cos(angle), jnp.cos(angle)], -1)
-    sine = jnp.concatenate([-jnp.sin(angle), jnp.sin(angle)], -1)
+    rate = jnp.concatenate([inverse, inverse])[None, :]
     bf16, f32 = jnp.bfloat16, jnp.float32
     dma = pltpu.SemaphoreType.DMA
     spec = pl.BlockSpec(memory_space=pltpu.VMEM)
     out = pl.pallas_call(
         functools.partial(layer_kernel, n_seq, n_head, kv_heads, groups, reach),
         out_shape=jax.ShapeDtypeStruct((width, rows), bf16),
-        in_specs=[pl.BlockSpec(memory_space=pl.ANY)] * 8,
+        in_specs=[pl.BlockSpec(memory_space=pltpu.MemorySpace.HBM)] * 8,
         out_specs=spec,
         scratch_shapes=[
             pltpu.VMEM(queries.shape, bf16), pltpu.VMEM(keys.shape, bf16), pltpu.VMEM(keys.shape, bf16),
-            pltpu.VMEM((rows, size), f32), pltpu.VMEM((rows, size), f32), pltpu.VMEM(out_weight.shape[::-1], bf16),
-            pltpu.VMEM((1, width), f32), pltpu.VMEM((width, rows), bf16), dma((8,)),
+            pltpu.VMEM((rows,), jnp.int32), pltpu.VMEM((1, size), f32), pltpu.VMEM(out_weight.shape[::-1], bf16),
+            pltpu.VMEM((width,), f32), pltpu.VMEM((width, rows), bf16), dma((8,)),
+            pltpu.VMEM((rows, size), f32), pltpu.VMEM((rows, size), f32),
             pltpu.VMEM((kv_heads * groups, rows, size), bf16),
             pltpu.VMEM((width, LANES), f32),
             pltpu.VMEM((kv_heads, (reach + 1) * rows, size), bf16),
@@ -498,7 +505,7 @@
             dma((n_head,)), dma((n_head,)),
         ],
         compiler_params=pltpu.CompilerParams(has_side_effects=True, collective_id=0, vmem_limit_bytes=44 * 1024 * 1024),
-    )(queries, keys, values, cosine, sine, out_weight.T, post_gain[None, :], residual.T)
+    )(*[pltpu.with_memory_space_constraint(x, pltpu.MemorySpace.HBM) for x in (queries, keys, values, positions, rate, out_weight.T, post_gain, residual.T)])
     return out.T
 
 

time: 126 us -> 117 us (0.929)
  the two profiles are of different devices: /device:TPU:0 before, /device:TPU:3 now
where the time goes in v3:
time: 117 us
  Pallas kernels  116 us (99%)
    pallas_call x1, Pallas kernels, fused(): pl.pallas_call(functools.partial(layer_kernel, n_seq, n_head, kv_heads, g...  116 us

profile of v3, /device:TPU:3, one launch (start us, length us, event | category | flops | bytes accessed | tf_op | source)
XLA Modules:
  0.0 117.2 jit_solution(11613572898886345667)
XLA Ops:
  0.0 0.6 maximum_bitcast_fusion.rate_hbm
  0.6 115.5 %shard_map.73 = bf16[1344,512]{1,0:T(8,128)(2,1)S(1)} custom-call(bf16[512,8,128]{2,1,0:T(8,128)(2,1)} %q_hbm.1, bf16[512,4,128]{2,1,0:T(4,128)(2,1)} %k_hbm.1, bf16[512,4,128]{2,1,0:T(4,128)(2,1)} %v_hbm.1, s32[512]{0:T(512)} %pos_hbm.1, f32[1,128]{1,0:T(1,128)} %maximum_bitcast_fusion.rate_hbm, bf16[672,1024]{1,0:T(8,128)(2,1)} %bitcast.6, f32[1344]{0:T(1024)} %gain_hbm.1, ...), custom_call_target="tpu_custom_call" | custom-call | tf_op jit(solution)/shard_map/pallas_call | solution.py:482
  116.2 1.1 copy.9
  (1 shorter events, 0.0 us)

commit v4 on v3

--- a/solution.py
+++ b/solution.py
@@ -25,10 +25,9 @@
 )
 PLAN = (
     "T6", "T4", "T0", "T1", "T5", "T2", "T3", "C0", "A0", "A1", "A2", "A3",
-    "C1", "C2", "C3", "R10", "R11", "R12", "R13", "X0", "Y0", "D0", "S0", "P002",
-    "R20", "R21", "P022", "R22", "R23", "R31", "X1", "Y1", "D1", "S1", "P102", "R30",
-    "P122", "R32", "R33", "X2", "Y2", "D2", "S2", "P202", "P222", "X3", "Y3", "D3",
-    "S3", "P302", "P32", "P33",
+    "C1", "C2", "C3", "R10", "R11", "R12", "R13", "R20", "R21", "X0", "Y0", "D0",
+    "S0", "P004", "R22", "R23", "R30", "R31", "X1", "Y1", "D1", "S1", "P104", "R32",
+    "R33", "X2", "Y2", "D2", "S2", "P204", "X3", "Y3", "D3", "S3", "P303", "P33",
 )
 DIRECT = (0, 1, 2, 3, )
 
@@ -341,6 +340,20 @@
         cos_ref[t : t + size, :] = jnp.cos(angle)
         sine = jnp.sin(angle)
         sin_ref[t : t + size, :] = jnp.where(early, -sine, sine)
+    loads[4].wait()
+    pl.semaphore_wait(barrier, n_seq + n_head - 2)
+
+    @pl.when(me // sub == z)
+    def _():
+        own_copy().start()
+
+    @pl.when(me // sub != z)
+    def _():
+        own_climb().start()
+
+    for word in LAUNCH:
+        if word[0] != "H":
+            scatter(others[int(word[1])])
     for load in loads[2:4]:
         load.wait()
     for t in range(0, rows, part):
@@ -348,23 +361,8 @@
         k_ext[:, span + t : span + t + part, :] = turned(k_raw[t : t + part])
     for g in range(kv_heads):
         v_ext[g, :, span : span + rows] = v_raw[:, g, :].T
-    loads[4].wait()
-    pl.semaphore_wait(barrier, n_seq + n_head - 2)
-
-    @pl.when(me // sub == z)
-    def _():
-        own_copy().start()
-
-    @pl.when(me // sub != z)
-    def _():
-        own_climb().start()
-
-    for word in LAUNCH:
-        if word[0] == "H":
-            start_halo(int(word[1]))
-        else:
-            scatter(others[int(word[1])])
-
+    for g in range(kv_heads):
+        start_halo(g)
     squares[0] = jnp.zeros((8, rows), jnp.float32)
     loads[5].wait()
     for t in range(0, rows, part):

time: 117 us -> 114 us (0.974)
  the two profiles are of different devices: /device:TPU:3 before, /device:TPU:7 now
where the time goes in v4:
time: 114 us
  Pallas kernels  112 us (98%)
    pallas_call x1, Pallas kernels, fused(): pl.pallas_call(functools.partial(layer_kernel, n_seq, n_head, kv_heads, g...  112 us

profile of v4, /device:TPU:7, one launch (start us, length us, event | category | flops | bytes accessed | tf_op | source)
XLA Modules:
  0.0 114.2 jit_solution(6959716501816814946)
XLA Ops:
  0.0 0.6 maximum_bitcast_fusion.rate_hbm
  0.6 112.5 %shard_map.73 = bf16[1344,512]{1,0:T(8,128)(2,1)S(1)} custom-call(bf16[512,8,128]{2,1,0:T(8,128)(2,1)} %q_hbm.1, bf16[512,4,128]{2,1,0:T(4,128)(2,1)} %k_hbm.1, bf16[512,4,128]{2,1,0:T(4,128)(2,1)} %v_hbm.1, s32[512]{0:T(512)} %pos_hbm.1, f32[1,128]{1,0:T(1,128)} %maximum_bitcast_fusion.rate_hbm, bf16[672,1024]{1,0:T(8,128)(2,1)} %bitcast.6, f32[1344]{0:T(1024)} %gain_hbm.1, ...), custom_call_target="tpu_custom_call" | custom-call | tf_op jit(solution)/shard_map/pallas_call | solution.py:480
  113.1 1.1 copy.9
  (1 shorter events, 0.0 us)

commit v5 on v4

--- a/solution.py
+++ b/solution.py
@@ -21,12 +21,12 @@
 LANES = 128
 MESH = pl.DeviceIdType.MESH
 LAUNCH = (
-    "Z4", "Z0", "Z1", "Z5", "Z2", "Z3", "Z6", "H0", "H1", "H2", "H3",
+    "Z4", "Z0", "Z1", "Z2", "Z3", "Z5", "Z6", "H0", "H1", "H2", "H3",
 )
 PLAN = (
-    "T6", "T4", "T0", "T1", "T5", "T2", "T3", "C0", "A0", "A1", "A2", "A3",
+    "T6", "T4", "T0", "T1", "T2", "T3", "T5", "C0", "A0", "A1", "A2", "A3",
     "C1", "C2", "C3", "R10", "R11", "R12", "R13", "R20", "R21", "X0", "Y0", "D0",
-    "S0", "P004", "R22", "R23", "R30", "R31", "X1", "Y1", "D1", "S1", "P104", "R32",
+    "S0", "R22", "R23", "P004", "R30", "R31", "R32", "X1", "Y1", "D1", "S1", "P104",
     "R33", "X2", "Y2", "D2", "S2", "P204", "X3", "Y3", "D3", "S3", "P303", "P33",
 )
 DIRECT = (0, 1, 2, 3, )
@@ -393,20 +393,6 @@
 
     for d in range(1, n_head):
         sq(d, lax.rem(z + d, n_head)).start()
-    for d in range(1, n_head):
-        sq(d, z).wait_recv()
-    loads[7].wait()
-    whole = jnp.sum(jnp.sum(squares[...], axis=0), axis=0, keepdims=True)
-    inverse = lax.rsqrt(whole / (n_head * sub * feats) + EPS)
-    for j in range(sub):
-        at = pl.ds(j * feats, feats)
-        gain = jnp.concatenate([gain_col[at, :]] * (rows // LANES), 1)
-        out_ref[at, :] = (
-            res_ref[at, :].astype(jnp.float32) + gain * (acc[j] * inverse)
-        ).astype(jnp.bfloat16)
-
-    for d in range(1, n_head):
-        sq(d, z).wait_send()
     for g in range(kv_heads):
         for dist in range(1, reach + 1):
             leaves = me + dist < n_seq
@@ -448,6 +434,20 @@
             @pl.when(jnp.logical_and(r >= z, z >= 1))
             def _():
                 ctx_down(r, g).wait_send()
+    for d in range(1, n_head):
+        sq(d, z).wait_recv()
+    loads[7].wait()
+    whole = jnp.sum(jnp.sum(squares[...], axis=0), axis=0, keepdims=True)
+    inverse = lax.rsqrt(whole / (n_head * sub * feats) + EPS)
+    for j in range(sub):
+        at = pl.ds(j * feats, feats)
+        gain = jnp.concatenate([gain_col[at, :]] * (rows // LANES), 1)
+        out_ref[at, :] = (
+            res_ref[at, :].astype(jnp.float32) + gain * (acc[j] * inverse)
+        ).astype(jnp.bfloat16)
+
+    for d in range(1, n_head):
+        sq(d, z).wait_send()
 
 
 def fits(rows, heads_rows, kv_heads, groups, feats, n_seq, n_head):

time: 114 us -> 114 us (level)
  no operation moved by 1% of the time
where the time goes in v5:
time: 114 us
  Pallas kernels  112 us (98%)
    pallas_call x1, Pallas kernels, fused(): pl.pallas_call(functools.partial(layer_kernel, n_seq, n_head, kv_heads, g...  112 us

profile of v5, /device:TPU:7, one launch (start us, length us, event | category | flops | bytes accessed | tf_op | source)
XLA Modules:
  0.0 114.0 jit_solution(4510753985617549622)
XLA Ops:
  0.0 0.6 maximum_bitcast_fusion.rate_hbm
  0.6 112.3 %shard_map.73 = bf16[1344,512]{1,0:T(8,128)(2,1)S(1)} custom-call(bf16[512,8,128]{2,1,0:T(8,128)(2,1)} %q_hbm.1, bf16[512,4,128]{2,1,0:T(4,128)(2,1)} %k_hbm.1, bf16[512,4,128]{2,1,0:T(4,128)(2,1)} %v_hbm.1, s32[512]{0:T(512)} %pos_hbm.1, f32[1,128]{1,0:T(1,128)} %maximum_bitcast_fusion.rate_hbm, bf16[672,1024]{1,0:T(8,128)(2,1)} %bitcast.6, f32[1344]{0:T(1024)} %gain_hbm.1, ...), custom_call_target="tpu_custom_call" | custom-call | tf_op jit(solution)/shard_map/pallas_call | solution.py:480
  112.9 1.1 copy.9
  (1 shorter events, 0.0 us)

commit v6 on v5

--- a/solution.py
+++ b/solution.py
@@ -290,7 +290,7 @@
         def _():
             ctx_down(z, g).start()
 
-    tile = next(t for t in range(256, 0, -16) if feats % t == 0)
+    tile = next(t for t in range(feats, 0, -16) if feats % t == 0)
 
     def project(s, g, n=1):
         last = s == n_head - 1 and g + n == kv_heads

time: 114 us -> 113 us (level)
  the two profiles are of different devices: /device:TPU:7 before, /device:TPU:0 now
where the time goes in v6:
time: 113 us; the launch traced here: 111 us
  Pallas kernels  109 us (96%)
    pallas_call x1, Pallas kernels, fused(): pl.pallas_call(functools.partial(layer_kernel, n_seq, n_head, kv_heads, g...  109 us

profile of v6, /device:TPU:0, one launch (start us, length us, event | category | flops | bytes accessed | tf_op | source)
XLA Modules:
  0.0 110.6 jit_solution(3314057065791385030)
XLA Ops:
  0.0 0.6 maximum_bitcast_fusion.rate_hbm
  0.6 108.9 %shard_map.73 = bf16[1344,512]{1,0:T(8,128)(2,1)S(1)} custom-call(bf16[512,8,128]{2,1,0:T(8,128)(2,1)} %q_hbm.1, bf16[512,4,128]{2,1,0:T(4,128)(2,1)} %k_hbm.1, bf16[512,4,128]{2,1,0:T(4,128)(2,1)} %v_hbm.1, s32[512]{0:T(512)} %pos_hbm.1, f32[1,128]{1,0:T(1,128)} %maximum_bitcast_fusion.rate_hbm, bf16[672,1024]{1,0:T(8,128)(2,1)} %bitcast.6, f32[1344]{0:T(1024)} %gain_hbm.1, ...), custom_call_target="tpu_custom_call" | custom-call | tf_op jit(solution)/shard_map/pallas_call | solution.py:480
  109.5 1.1 copy.9
  (1 shorter events, 0.0 us)

commit v7 on v6

--- a/solution.py
+++ b/solution.py
@@ -27,7 +27,7 @@
     "T6", "T4", "T0", "T1", "T2", "T3", "T5", "C0", "A0", "A1", "A2", "A3",
     "C1", "C2", "C3", "R10", "R11", "R12", "R13", "R20", "R21", "X0", "Y0", "D0",
     "S0", "R22", "R23", "P004", "R30", "R31", "R32", "X1", "Y1", "D1", "S1", "P104",
-    "R33", "X2", "Y2", "D2", "S2", "P204", "X3", "Y3", "D3", "S3", "P303", "P33",
+    "R33", "X2", "Y2", "D2", "S2", "P204", "X3", "Y3", "D3", "S3", "P302", "P322",
 )
 DIRECT = (0, 1, 2, 3, )
 

time: 113 us -> 113 us (level)
  no operation moved by 1% of the time
where the time goes in v7:
time: 113 us; the launch traced here: 111 us
  Pallas kernels  109 us (96%)
    pallas_call x1, Pallas kernels, fused(): pl.pallas_call(functools.partial(layer_kernel, n_seq, n_head, kv_heads, g...  109 us

profile of v7, /device:TPU:0, one launch (start us, length us, event | category | flops | bytes accessed | tf_op | source)
XLA Modules:
  0.0 111.0 jit_solution(550067491043405244)
XLA Ops:
  0.0 0.6 maximum_bitcast_fusion.rate_hbm
  0.6 109.3 %shard_map.73 = bf16[1344,512]{1,0:T(8,128)(2,1)S(1)} custom-call(bf16[512,8,128]{2,1,0:T(8,128)(2,1)} %q_hbm.1, bf16[512,4,128]{2,1,0:T(4,128)(2,1)} %k_hbm.1, bf16[512,4,128]{2,1,0:T(4,128)(2,1)} %v_hbm.1, s32[512]{0:T(512)} %pos_hbm.1, f32[1,128]{1,0:T(1,128)} %maximum_bitcast_fusion.rate_hbm, bf16[672,1024]{1,0:T(8,128)(2,1)} %bitcast.6, f32[1344]{0:T(1024)} %gain_hbm.1, ...), custom_call_target="tpu_custom_call" | custom-call | tf_op jit(solution)/shard_map/pallas_call | solution.py:480
  109.9 1.1 copy.9
  (1 shorter events, 0.0 us)
